TPU v7x, 32 devices: a whole 2x2x4 slice. The times are simulated.
32 devices in a mesh: date: 4 (over y, x), path: 8 (over z, core).
Axes of the slice: x: 2, y: 2, z: 4, core: 2. Of those that a mesh axis runs over, the one named last changes fastest.
Arguments:
- factors: bfloat16 [32, 16, 32768], P('date', None, 'path'), may hold values from -10 to 10
- cashflows: bfloat16 [32, 64, 32768], P('date', None, 'path'), may hold values from -12 to 12
- frequency: bfloat16 [128, 16], replicated, may hold values from -1.5 to 1.5
- phases: float32 [128], replicated, may hold values from -3.140625 to 3.140625
- margin_lag: int32 [64], replicated, may hold values from 1 to 2
- thresholds: int32 [64], replicated, may hold values from 0 to 149
- transfer_min: int32 [64], replicated, may hold values from 0 to 59
Outputs:
- exposure: bfloat16 [32, 64, 32768], P('date', None, 'path')
- profile: float32 [32, 64], P('date')
All inputs are finite; a program needn't handle non-finite values.
Results may differ from a plain program's by a relative error of at most 0.0058.
Values may be sent and summed in bfloat16 or wider, within the bound.
A program may use at most 128 MiB of HBM per device.

v0:
```python
import jax
import jax.numpy as jnp
from jax import lax
from jax.experimental import pallas as pl
from jax.experimental.pallas import tpu as pltpu
from jax.sharding import PartitionSpec as P

LAG_MAX = 2


ridge_weight = 0.05
inverse_turn = 0.15915494309189535
wave = (
    1.414213547,
    -27.91545067,
    91.83777847,
    -120.8447093,
    85.08959522,
    -36.72272039,
    9.231570304,
)


def shifted_2(value, axis, by):
    length = lax.axis_size(axis)
    pairs = [(i, i + by) for i in range(length) if 0 <= i + by < length]
    return lax.ppermute(value, axis, pairs)


def featurize(frequency, phases, factors):
    angles = jnp.einsum("kr,trp->tkp", frequency, factors, preferred_element_type=jnp.float32)
    turns = (angles + phases[None, :, None]) * inverse_turn
    turns = turns - jnp.round(turns)
    square = turns * turns
    total = wave[-1]
    for term in wave[-2::-1]:
        total = total * square + term
    return total.astype(jnp.bfloat16)


def eliminate(scale, gram_ref, right_ref, out_ref, left, right):
    dates, size, _ = gram_ref.shape
    rows = lax.broadcasted_iota(jnp.int32, (size, size), 0)
    columns = lax.broadcasted_iota(jnp.int32, (size, size), 1)
    ridge = jnp.where(rows == columns, ridge_weight, 0.0)
    for d in range(dates):
        left[d] = gram_ref[d] * scale + ridge
        right[d] = right_ref[d] * scale

    def step(j, carry):
        place = jnp.full((size, size), j, jnp.int32)
        scaled = []
        for d in range(dates):
            row = left[d, pl.ds(j, 1), :]
            pivot = jnp.take_along_axis(
                jnp.broadcast_to(row, (8, size)), place[:8], axis=1, mode="promise_in_bounds"
            )
            inverse = (1.0 / pivot)[:1]
            row_right = right[d, pl.ds(j, 1), :] * inverse[:, : right.shape[2]]
            scaled.append((row * inverse, row_right))
        for d, (row, row_right) in enumerate(scaled):
            for first in range(0, size, 8):
                band = pl.ds(first, 8)
                column = jnp.take_along_axis(
                    left[d, band, :], place[:8], axis=1, mode="promise_in_bounds"
                )
                left[d, band, :] = left[d, band, :] - column * row
                right[d, band, :] = right[d, band, :] - column[:, : right.shape[2]] * row_right
        for d, (row, row_right) in enumerate(scaled):
            left[d, pl.ds(j, 1), :] = row
            right[d, pl.ds(j, 1), :] = row_right
        return carry

    lax.fori_loop(0, size, step, 0)
    for d in range(dates):
        out_ref[d] = right[d].astype(out_ref.dtype)


def regress(gram_sum, right_sum, paths_all):
    def kernel(*refs):
        eliminate(1.0 / paths_all, *refs)

    return pl.pallas_call(
        kernel,
        out_shape=jax.ShapeDtypeStruct(right_sum.shape, jnp.bfloat16),
        in_specs=[pl.BlockSpec(memory_space=pltpu.VMEM)] * 2,
        out_specs=pl.BlockSpec(memory_space=pltpu.VMEM),
        scratch_shapes=[
            pltpu.VMEM(gram_sum.shape, jnp.float32),
            pltpu.VMEM(right_sum.shape, jnp.float32),
        ],
    )(gram_sum, right_sum)


def fitted(coefficients, features):
    return jnp.einsum(
        "tkn,tkp->tnp", coefficients, features, preferred_element_type=jnp.float32
    ).astype(jnp.bfloat16)


def local(factors, cashflows, frequency, phases, margin_lag, thresholds, transfer_min):
    prior_factors = shifted_2(factors[-LAG_MAX:], "date", 1)
    features = featurize(frequency, phases, factors)
    gram_sum = jnp.einsum("tkp,tjp->tkj", features, features, preferred_element_type=jnp.float32)
    right_sum = jnp.einsum("tkp,tnp->tkn", features, cashflows, preferred_element_type=jnp.float32)
    gram_sum, right_sum = lax.psum((gram_sum, right_sum), "path")
    prior_features = featurize(frequency, phases, prior_factors)
    paths_all = features.shape[2] * lax.axis_size("path")
    coefficients = regress(gram_sum, right_sum, paths_all)
    prior_coefficients = shifted_2(coefficients[-LAG_MAX:], "date", 1)
    values = fitted(coefficients, features)
    prior_values = fitted(prior_coefficients, prior_features)
    joined = jnp.concatenate([prior_values, values], axis=0)
    dates_here = values.shape[0]
    lagged = jnp.zeros(values.shape, jnp.float32)
    for lag_value in range(1, LAG_MAX + 1):
        shifted = joined[LAG_MAX - lag_value : LAG_MAX - lag_value + dates_here].astype(jnp.float32)
        lagged = jnp.where((margin_lag == lag_value)[None, :, None], shifted, lagged)
    offset = (thresholds + transfer_min).astype(jnp.float32) / 100.0
    collateral = jnp.maximum(lagged - offset[None, :, None], 0.0)
    exposure = jnp.maximum(values.astype(jnp.float32) - collateral, 0.0)
    profile = lax.psum(jnp.sum(exposure, axis=2), "path") / paths_all
    return (exposure.astype(jnp.bfloat16), profile)


def solution(mesh):
    return jax.shard_map(
        local,
        mesh=mesh,
        in_specs=(P("date", None, "path"), P("date", None, "path"), P(), P(), P(), P(), P()),
        out_specs=(P("date", None, "path"), P("date", None)),
        check_vma=False,
    )
```

profile of v0, /device:TPU:5, one launch (start us, length us, event | category | flops | bytes accessed | tf_op | source)
XLA Modules:
  0.0 167.9 jit_solution(267144450831073917)
XLA Ops:
  7.2 0.0 copy-start
  7.2 0.0 all-reduce.3.cloned.1.call-start
  7.2 1.0 slice.13
  8.2 3.1 %collective-permute-start.1 = (bf16[2,16,4096]{2,1,0:T(8,128)(2,1)S(1)}, bf16[2,16,4096]{2,1,0:T(8,128)(2,1)S(1)}, u32[]{:S(2)}, u32[]{:S(2)}) collective-permute-start(bf16[2,16,4096]{2,1,0:T(8,128)(2,1)S(1)} %slice.13), channel_id=1, source_target_pairs={{0,8},{8,16},{16,24},{1,9},{9,17},{17,25},{2,10},{10,18},{18,26},{... | collective-permute-start | bytes 786440 | tf_op jit(solution)/shard_map/ppermute | solution.py:27
  11.3 0.0 copy-done
  11.3 11.6 %add_convert_fusion = bf16[8,128,4096]{1,2,0:T(8,128)(2,1)S(1)} fusion(bf16[8,16,4096]{2,1,0:T(8,128)(2,1)} %param.7, f32[128]{0:T(128)} %param.10, bf16[128,16]{0,1:T(8,128)(2,1)S(1)} %copy-done), kind=kOutput, calls=%fused_computation.2 | convolution fusion | flops 209715200 | bytes 9441792 | tf_op jit(solution)/shard_map/kr,trp->tkp/dot_general | solution.py:31
  23.0 0.0 copy-start.1
  23.0 3.5 %fusion.17 = f32[8,128,128]{2,1,0:T(8,128)} fusion(bf16[8,128,4096]{1,2,0:T(8,128)(2,1)S(1)} %add_convert_fusion), kind=kOutput, calls=%fused_computation.31 | convolution fusion | flops 1073741824 | bytes 8912896 | tf_op jit(solution)/shard_map/tkp,tjp->tkj/dot_general | solution.py:104
  26.5 0.0 copy-done.1
  26.5 5.6 %fusion.18 = f32[8,128,64]{2,1,0:T(8,128)} fusion(bf16[8,128,4096]{1,2,0:T(8,128)(2,1)S(1)} %add_convert_fusion, bf16[8,64,4096]{2,1,0:T(8,128)(2,1)} %param.8), kind=kOutput, calls=%fused_computation.32 | convolution fusion | flops 536870912 | bytes 12845056 | tf_op jit(solution)/shard_map/tkp,tnp->tkn/dot_general | solution.py:105
  32.2 0.0 all-reduce.3.cloned.1.call-update
  32.2 0.0 copy-done.3
  32.2 0.0 copy-done.4
  32.3 58.2 %all-reduce.3.cloned.1.call-done = (f32[8,128,128]{2,1,0:T(8,128)}, f32[8,128,64]{2,1,0:T(8,128)}) async-done(((f32[8,128,128]{2,1,0:T(8,128)}, f32[8,128,64]{2,1,0:T(8,128)}), (f32[8,128,128]{2,1,0:T(8,128)}, f32[8,128,64]{2,1,0:T(8,128)})) %all-reduce.3.cloned.1.call-update) | async-done | bytes 786448 | tf_op jit(solution)/shard_map/psum | solution.py:106
  90.5 30.9 %shard_map.86 = bf16[8,128,64]{2,1,0:T(8,128)(2,1)} custom-call(f32[8,128,128]{2,1,0:T(8,128)} %get-tuple-element.2.refs_0_, f32[8,128,64]{2,1,0:T(8,128)} %get-tuple-element.3.refs_1_), custom_call_target="tpu_custom_call" | custom-call | tf_op jit(solution)/shard_map/pallas_call | solution.py:83
  121.4 0.8 slice.16
  122.2 3.3 %collective-permute-start = (bf16[2,128,64]{2,1,0:T(8,128)(2,1)S(1)}, bf16[2,128,64]{2,1,0:T(8,128)(2,1)S(1)}, u32[]{:S(2)}, u32[]{:S(2)}) collective-permute-start(bf16[2,128,64]{2,1,0:T(8,128)(2,1)S(1)} %slice.16), channel_id=1, source_target_pairs={{0,8},{8,16},{16,24},{1,9},{9,17},{17,25},{2,10},{10,18},{18,26},{... | collective-permute-start | bytes 98312 | tf_op jit(solution)/shard_map/ppermute | solution.py:27
  125.5 8.5 %convolution_convert_fusion = bf16[8,64,4096]{2,1,0:T(8,128)(2,1)} fusion(bf16[8,128,64]{2,1,0:T(8,128)(2,1)} %shard_map.86, bf16[8,128,4096]{1,2,0:T(8,128)(2,1)} %copy-done.1), kind=kOutput, calls=%fused_computation.5 | convolution fusion | flops 538968064 | bytes 12713984 | tf_op jit(solution)/shard_map/tkn,tkp->tnp/dot_general | solution.py:96
  134.0 0.0 collective-permute-done.1
  134.0 0.0 collective-permute-done
  134.0 2.9 %convolution_convert_fusion.1 = bf16[2,64,4096]{2,1,0:T(8,128)(2,1)S(1)} fusion(bf16[2,128,64]{2,1,0:T(8,128)(2,1)S(1)} %collective-permute-done, bf16[2,16,4096]{2,1,0:T(8,128)(2,1)S(1)} %collective-permute-done.1, f32[128]{0:T(128)S(1)} %copy-done.5, bf16[128,16]{0,1:T(8,128)(2,1)S(1)} %copy-done), kind=kOutput, calls=%fused_computation.12 | convolution fusion | flops 187170816 | bytes 1348096 | tf_op jit(solution)/shard_map/tkn,tkp->tnp/dot_general | solution.py:96
  137.0 7.9 %fusion.16 = (f32[8,64]{1,0:T(8,128)S(1)}, bf16[8,64,4096]{2,1,0:T(8,128)(2,1)}) fusion(f32[64]{0:T(128)S(1)} %convert_multiply_fusion, bf16[8,64,4096]{2,1,0:T(8,128)(2,1)} %convolution_convert_fusion, bf16[2,64,4096]{2,1,0:T(8,128)(2,1)S(1)} %convolution_convert_fusion.1, pred[64]{0:T(512)(128)(4,1)S(1)} %get-tuple-element.7, ...), kind=kLoop, calls=%fused_computation.30 | loop fusion | flops 27262464 | bytes 9439616 | tf_op jit(solution)/shard_map/reduce_sum | solution.py:122
  144.9 15.6 %psum.23 = f32[8,64]{1,0:T(8,128)S(1)} all-reduce(f32[8,64]{1,0:T(8,128)S(1)} %get-tuple-element.4), channel_id=1, replica_groups=mesh['date'=4,'path'=8] {'path'}, use_global_device_ids=true, to_apply=%region_3.4 | all-reduce | flops 512 | bytes 4096 | tf_op jit(solution)/shard_map/psum | solution.py:122
  160.5 0.6 broadcast_multiply_fusion
  (8 shorter events, 0.0 us)
Async XLA Ops:
  7.2 4.2 %copy-start = (bf16[128,16]{0,1:T(8,128)(2,1)S(1)}, bf16[128,16]{0,1:T(8,128)(2,1)}, u32[]{:S(2)}) copy-start(bf16[128,16]{0,1:T(8,128)(2,1)} %param.9) | copy-start | bytes 12292
  7.2 83.3 %all-reduce.3.cloned.1.call-start = ((), (), s32[]{:S(2)}) async-start(), calls=%async_computation | async-start | bytes 2097152 | tf_op jit(solution)/shard_map/psum | solution.py:106
  8.2 125.8 %collective-permute-start.1 = (bf16[2,16,4096]{2,1,0:T(8,128)(2,1)S(1)}, bf16[2,16,4096]{2,1,0:T(8,128)(2,1)S(1)}, u32[]{:S(2)}, u32[]{:S(2)}) collective-permute-start(bf16[2,16,4096]{2,1,0:T(8,128)(2,1)S(1)} %slice.13), channel_id=1, source_target_pairs={{0,8},{8,16},{16,24},{1,9},{9,17},{17,25},{2,10},{10,18},{18,26},{... | collective-permute-start | bytes 786440 | tf_op jit(solution)/shard_map/ppermute | solution.py:27
  23.0 3.6 %copy-start.1 = (bf16[8,128,4096]{1,2,0:T(8,128)(2,1)}, bf16[8,128,4096]{1,2,0:T(8,128)(2,1)S(1)}, u32[]{:S(2)}) copy-start(bf16[8,128,4096]{1,2,0:T(8,128)(2,1)S(1)} %add_convert_fusion) | copy-start | bytes 25165828
  26.5 5.7 %copy-start.2 = (s32[64]{0:T(128)S(1)}, s32[64]{0:T(128)}, u32[]{:S(2)}) copy-start(s32[64]{0:T(128)} %param.11) | copy-start | bytes 772
  26.5 5.7 %copy-start.3 = (s32[64]{0:T(128)S(1)}, s32[64]{0:T(128)}, u32[]{:S(2)}) copy-start(s32[64]{0:T(128)} %param.12) | copy-start | bytes 772
  26.5 5.7 %copy-start.4 = (s32[64]{0:T(128)S(1)}, s32[64]{0:T(128)}, u32[]{:S(2)}) copy-start(s32[64]{0:T(128)} %param.13) | copy-start | bytes 772
  32.2 101.8 %copy-start.5 = (f32[128]{0:T(128)S(1)}, f32[128]{0:T(128)}, u32[]{:S(2)}) copy-start(f32[128]{0:T(128)} %param.10) | copy-start | bytes 1540
  122.2 11.8 %collective-permute-start = (bf16[2,128,64]{2,1,0:T(8,128)(2,1)S(1)}, bf16[2,128,64]{2,1,0:T(8,128)(2,1)S(1)}, u32[]{:S(2)}, u32[]{:S(2)}) collective-permute-start(bf16[2,128,64]{2,1,0:T(8,128)(2,1)S(1)} %slice.16), channel_id=1, source_target_pairs={{0,8},{8,16},{16,24},{1,9},{9,17},{17,25},{2,10},{10,18},{18,26},{... | collective-permute-start | bytes 98312 | tf_op jit(solution)/shard_map/ppermute | solution.py:27
Sparse Core Ops, SparseCore 0:
  32.3 58.0 all-reduce.2
where the time goes:
time: 170 us; the launch traced here: 168 us
  waiting for transfers between devices  58.2 us (34%)
  matrix products  32.3 us (19%)
  Pallas kernels  30.9 us (18%)
  blocking collectives  15.6 us (9%)
  between operations  14.1 us (8%)
  other arithmetic  8.53 us (5%)
  starting transfers between devices  6.42 us (4%)
  local copies, waits for them, and re-layouts  1.84 us (1%)
    psum x1, waiting for transfers between devices, local(): gram_sum, right_sum = lax.psum((gram_sum, right_sum), 'path')  58.2 us
    pallas_call x1, Pallas kernels, regress(): pl.pallas_call(kernel, out_shape=jax.ShapeDtypeStruct(right_sum.shape, jn...  30.9 us
    psum x1, blocking collectives, local(): profile = lax.psum(jnp.sum(exposure, axis=2), 'path') / paths_all  15.6 us
    dot_general x1, matrix products, featurize(): jnp.einsum('kr,trp->tkp', frequency, factors, preferred_element_type=jnp....  11.6 us
    dot_general x2, matrix products, fitted(): jnp.einsum('tkn,tkp->tnp', coefficients, features, preferred_element_type...  11.4 us
    reduce_sum x1, other arithmetic, local(): profile = lax.psum(jnp.sum(exposure, axis=2), 'path') / paths_all  7.92 us
    ppermute x2, starting transfers between devices, shifted_2(): return lax.ppermute(value, axis, pairs)  6.39 us
    dot_general x1, matrix products, local(): jnp.einsum('tkp,tnp->tkn', features, cashflows, preferred_element_type=jn...  5.64 us
  transfers between devices with their start and end apart: 3, of which 1 were waited for; matrix products, arithmetic and copies ran while one was open for 18% of the time, Pallas kernels for 18%

commit v1 on v0

v1 whole, which is shorter than its diff:
```python
import functools

import jax
import jax.numpy as jnp
from jax import lax
from jax.experimental import pallas as pl
from jax.experimental.pallas import tpu as pltpu
from jax.sharding import PartitionSpec as P

LAG_MAX = 2
MESH = pl.DeviceIdType.MESH
f32 = jnp.float32
bf16 = jnp.bfloat16

ridge_weight = 0.05
inverse_turn = 0.15915494309189535
root_two = 1.4142135623730951
half_wave = (1.6817899533136271, -8.29873762982186, 6.809195244612708, -2.0985399883857303)
newton_steps = 8
FEATURE_WIDTH = 512
VALUE_WIDTH = 512


def split(x, parts):
    out = []
    for _ in range(parts):
        piece = x.astype(bf16)
        out.append(piece)
        x = x - piece.astype(f32)
    return out


def contract(left, right):
    return lax.dot_general(left, right, (((1,), (0,)), ((), ())), preferred_element_type=f32)


def contract_last(left, right):
    return lax.dot_general(left, right, (((1,), (1,)), ((), ())), preferred_element_type=f32)


def product(left, right):
    if len(left) == 2:
        lh, lm = left
        rh, rm = right
        return contract(
            jnp.concatenate([lh, lm, lh, lm], axis=1), jnp.concatenate([rh, rh, rm, rm], axis=0)
        )
    lh, lm, ll = left
    rh, rm, rl = right
    return contract(
        jnp.concatenate([lh, lm, ll, lh, lm, lh], axis=1),
        jnp.concatenate([rh, rh, rh, rm, rm, rl], axis=0),
    )


def solve(system, right):
    size = system.shape[0]
    rows = lax.broadcasted_iota(jnp.int32, (size, size), 0)
    columns = lax.broadcasted_iota(jnp.int32, (size, size), 1)
    identity = jnp.where(rows == columns, 1.0, 0.0).astype(f32)
    top = 2.0 * size + ridge_weight
    least = 0.99 * ridge_weight / top
    scaled = system * (1.0 / top)
    inverse = None
    for step in range(newton_steps):
        weight = 2.0 / (1.0 + least)
        factor = 2.0 * identity - weight * scaled
        last = step == newton_steps - 1
        if inverse is None:
            inverse = (weight / top) * factor
            scaled = weight * product(split(scaled, 2), split(factor, 2))
        else:
            stack = inverse if last else jnp.concatenate([inverse, scaled], axis=0)
            stack = weight * product(split(stack, 2), split(factor, 2))
            inverse = stack[:size]
            scaled = None if last else stack[size:]
        least = 4.0 * least / (1.0 + least) ** 2
    inverse = split(inverse * (2.0 / (1.0 + least)), 3)
    found = product(split(right, 3), inverse)
    rest = right - product(split(found, 3), split(system, 3))
    return found + product(split(rest, 2), inverse[:2])


def as_column(row, width):
    return jnp.broadcast_to(row, (width, row.shape[1])).T


def kernel(
    axes,
    factors,
    cashflows,
    frequency,
    phases,
    margin_lag,
    thresholds,
    transfer_min,
    exposure,
    profile,
    state,
    flows,
    features,
    partial_sum,
    pair_part,
    pair_total,
    gathered,
    own_coefficients,
    coefficients,
    profile_own,
    profile_all,
    flows_sem,
    prior_send,
    prior_recv,
    pair_send,
    pair_recv,
    owner_send,
    owner_recv,
    coefficients_send,
    coefficients_recv,
    profile_send,
    profile_recv,
):
    slabs, group = axes
    dates, risk, paths = factors.shape
    terms = frequency.shape[1]
    sets = cashflows.shape[1]
    half = (terms + sets) // 2
    spread = group // dates
    paths_all = paths * group
    slab = lax.axis_index("date")
    me = lax.axis_index("path")
    partner = me + 1 - 2 * lax.rem(me, 2)
    side = lax.rem(me, 2)
    first = (2 * lax.div(me, 2)) // spread
    near = max(1, (2 * dates) // group)
    has_prior = slab > 0
    has_next = slab < slabs - 1

    def device(slab_index, path_index):
        return (slab_index, path_index)

    def date_at(step):
        return lax.rem(first + near + step, dates)

    def step_of(date):
        return lax.rem(date - first - near + 2 * dates, dates)

    barrier = pltpu.get_barrier_semaphore()

    def greet(j, carry):
        @pl.when(j != me)
        def _():
            pl.semaphore_signal(barrier, inc=1, device_id=device(slab, j), device_id_type=MESH)

        @pl.when(has_prior)
        def _():
            pl.semaphore_signal(barrier, inc=1, device_id=device(slab - 1, j), device_id_type=MESH)

        @pl.when(has_next)
        def _():
            pl.semaphore_signal(barrier, inc=1, device_id=device(slab + 1, j), device_id_type=MESH)

        return carry

    def flows_copy(step):
        return pltpu.make_async_copy(
            cashflows.at[date_at(step)], flows.at[step], flows_sem.at[step]
        )

    def load(step, carry):
        flows_copy(step).start()
        return carry

    lax.fori_loop(0, dates, load, 0)
    lax.fori_loop(0, group, greet, 0)

    turn = split(frequency[...].astype(f32).T * inverse_turn, 3)
    phase = split(as_column(phases[...] * inverse_turn, terms), 3)
    lane = lax.broadcasted_iota(jnp.int32, (terms, risk), 1)
    offset_part = jnp.zeros((terms, risk), f32)
    for i, piece in enumerate(phase):
        offset_part = jnp.where(lane == i, piece.astype(f32)[:, :risk], offset_part)
    wave_map = jnp.concatenate([piece.astype(f32) for piece in turn] + [offset_part], axis=1)
    wave_map = wave_map.astype(bf16)

    def featurize(source, date, slot, first_column):
        columns = pl.ds(first_column, FEATURE_WIDTH)
        now = source[date, :, columns]
        stacked = jnp.concatenate([now, now, now, jnp.ones(now.shape, bf16)], axis=0)
        turns = contract(wave_map, stacked)
        turns = turns - jnp.round(turns)
        square = turns * turns
        total = half_wave[-1]
        for term in half_wave[-2::-1]:
            total = total * square + term
        features[slot, :, columns] = (total * total - root_two).astype(bf16)

    def pair_copy(step):
        there = pl.ds(pl.multiple_of((1 - side) * half, 8), half)
        return pltpu.make_async_remote_copy(
            src_ref=partial_sum.at[step, there],
            dst_ref=pair_part.at[step],
            send_sem=pair_send.at[step],
            recv_sem=pair_recv.at[step],
            device_id=device(slab, partner),
            device_id_type=MESH,
        )

    def owner_copy(step, owner, slot):
        return pltpu.make_async_remote_copy(
            src_ref=pair_total.at[step],
            dst_ref=gathered.at[slot],
            send_sem=owner_send.at[step],
            recv_sem=owner_recv.at[slot],
            device_id=device(slab, owner),
            device_id_type=MESH,
        )

    def deliver(step):
        here = pl.ds(pl.multiple_of(side * half, 8), half)
        owner = date_at(step) * spread
        pair_copy(step).wait_recv()
        total = partial_sum[step, here] + pair_part[step]

        @pl.when(owner == me)
        def _():
            gathered[me] = total

        @pl.when(owner != me)
        def _():
            pair_total[step] = total
            owner_copy(step, owner, me).start()

    def prior_copy(target):
        return pltpu.make_async_remote_copy(
            src_ref=factors.at[pl.ds(dates - LAG_MAX, LAG_MAX)],
            dst_ref=state,
            send_sem=prior_send,
            recv_sem=prior_recv,
            device_id=device(target, me),
            device_id_type=MESH,
        )

    def gram(step):
        slot = LAG_MAX + step
        total = None
        for column in range(0, paths, FEATURE_WIDTH):
            featurize(factors, date_at(step), slot, column)
            columns = pl.ds(column, FEATURE_WIDTH)
            now = features[slot, :, columns]
            both = jnp.concatenate([now, flows[step, :, columns]], axis=0)
            part = contract_last(both, now)
            total = part if total is None else total + part
        partial_sum[step] = total

    def forward(step, carry):
        flows_copy(step).wait()
        gram(step)

        @pl.when(step == 0)
        def _():
            neighbours = (slab + slabs - 1) // slabs + (2 * slabs - 2 - slab) // slabs
            pl.semaphore_wait(barrier, group - 1 + group * neighbours)

        pair_copy(step).start()

        @pl.when(step > 0)
        def _():
            deliver(step - 1)

        return carry

    lax.fori_loop(0, dates, forward, 0)

    @pl.when(has_next)
    def _():
        prior_copy(slab + 1).start()

    deliver(dates - 1)

    @pl.when(has_prior)
    def _():
        prior_copy(slab).wait_recv()

        def prior(slot, carry):
            for column in range(0, paths, FEATURE_WIDTH):
                featurize(state, slot, slot, column)
            return carry

        lax.fori_loop(0, LAG_MAX, prior, 0)

    @pl.when(jnp.logical_not(has_prior))
    def _():
        features[pl.ds(0, LAG_MAX)] = jnp.zeros((LAG_MAX,) + features.shape[1:], bf16)
        coefficients[pl.ds(0, LAG_MAX)] = jnp.zeros((LAG_MAX, sets, terms), bf16)

    def coefficients_copy(target, j, slot, sem):
        return pltpu.make_async_remote_copy(
            src_ref=own_coefficients,
            dst_ref=coefficients.at[slot],
            send_sem=coefficients_send.at[sem],
            recv_sem=coefficients_recv.at[slot],
            device_id=device(target, j),
            device_id_type=MESH,
        )

    own = lax.div(me, spread)
    is_owner = lax.rem(me, spread) == 0
    tell_next = jnp.logical_and(
        jnp.logical_and(is_owner, has_next), own >= dates - LAG_MAX
    )

    @pl.when(is_owner)
    def _():
        def arrived(j, carry):
            @pl.when(j != me)
            def _():
                owner_copy(0, me, j).wait_recv()

            return carry

        lax.fori_loop(0, group, arrived, 0)
        upper = gathered[0]
        lower = gathered[1]
        for j in range(2, group, 2):
            upper = upper + gathered[j]
            lower = lower + gathered[j + 1]
        sums = jnp.concatenate([upper, lower], axis=0) * (1.0 / paths_all)
        rows = lax.broadcasted_iota(jnp.int32, (terms, terms), 0)
        columns = lax.broadcasted_iota(jnp.int32, (terms, terms), 1)
        system = sums[:terms] + jnp.where(rows == columns, ridge_weight, 0.0)
        answer = solve(system, sums[terms:]).astype(bf16)
        own_coefficients[...] = answer
        coefficients[LAG_MAX + own] = answer

        def tell(j, carry):
            @pl.when(j != me)
            def _():
                coefficients_copy(slab, j, LAG_MAX + own, j).start()

            return carry

        lax.fori_loop(0, group, tell, 0)

    @pl.when(tell_next)
    def _():
        def tell(j, carry):
            coefficients_copy(slab + 1, j, own - (dates - LAG_MAX), group + j).start()
            return carry

        lax.fori_loop(0, group, tell, 0)

    def arrived_coefficients(date, carry):
        @pl.when(date * spread != me)
        def _():
            coefficients_copy(slab, me, LAG_MAX + date, 0).wait_recv()

        return carry

    lax.fori_loop(0, dates, arrived_coefficients, 0)

    @pl.when(has_prior)
    def _():
        for i in range(LAG_MAX):
            coefficients_copy(slab, me, i, 0).wait_recv()

    lag = as_column(margin_lag[...].astype(f32), 128)
    offset = as_column((thresholds[...] + transfer_min[...]).astype(f32) / 100.0, 128)
    repeat = VALUE_WIDTH // 128
    lag = jnp.concatenate([lag] * repeat, axis=1)
    offset = jnp.concatenate([offset] * repeat, axis=1)

    def expose(block, totals):
        columns = pl.ds(pl.multiple_of(block * VALUE_WIDTH, VALUE_WIDTH), VALUE_WIDTH)
        earlier = []
        new_totals = []
        for date in range(-LAG_MAX, dates):
            slot = LAG_MAX + date if date < 0 else LAG_MAX + step_of(date)
            value = contract(coefficients[LAG_MAX + date], features[slot, :, columns])
            value = value.astype(bf16)
            if date >= 0:
                lagged = jnp.zeros(value.shape, f32)
                for lag_value in range(1, LAG_MAX + 1):
                    lagged = jnp.where(
                        lag == lag_value, earlier[-lag_value].astype(f32), lagged
                    )
                collateral = jnp.maximum(lagged - offset, 0.0)
                open_value = jnp.maximum(value.astype(f32) - collateral, 0.0)
                exposure[date, :, columns] = open_value.astype(bf16)
                total = totals[date]
                for i in range(repeat):
                    total = total + open_value[:, 128 * i : 128 * (i + 1)]
                new_totals.append(total)
            earlier.append(value)
        return tuple(new_totals)

    blocks = paths // VALUE_WIDTH
    totals = tuple(jnp.zeros((sets, 128), f32) for _ in range(dates))
    totals = lax.fori_loop(0, blocks, expose, totals)
    rows = [jnp.sum(total.T, axis=0, keepdims=True) for total in totals]
    profile_own[...] = jnp.concatenate(rows, axis=0)

    def profile_copy(j, slot):
        return pltpu.make_async_remote_copy(
            src_ref=profile_own,
            dst_ref=profile_all.at[slot],
            send_sem=profile_send.at[j],
            recv_sem=profile_recv.at[slot],
            device_id=device(slab, j),
            device_id_type=MESH,
        )

    def share(j, carry):
        @pl.when(j != me)
        def _():
            profile_copy(j, me).start()

        return carry

    lax.fori_loop(0, group, share, 0)
    profile_all[me] = profile_own[...]

    def received(j, carry):
        @pl.when(j != me)
        def _():
            profile_copy(0, j).wait_recv()

        return carry

    lax.fori_loop(0, group, received, 0)
    total = profile_all[0]
    for j in range(1, group):
        total = total + profile_all[j]
    profile[...] = total * (1.0 / paths_all)

    def sent(step, carry):
        pair_copy(step).wait_send()

        @pl.when(date_at(step) * spread != me)
        def _():
            owner_copy(step, me, me).wait_send()

        return carry

    lax.fori_loop(0, dates, sent, 0)

    def told(j, carry):
        @pl.when(j != me)
        def _():
            profile_copy(j, me).wait_send()

            @pl.when(is_owner)
            def _():
                coefficients_copy(slab, me, 0, j).wait_send()

        @pl.when(tell_next)
        def _():
            coefficients_copy(slab, me, 0, group + j).wait_send()

        return carry

    lax.fori_loop(0, group, told, 0)

    @pl.when(has_next)
    def _():
        prior_copy(slab).wait_send()


def local(axes, factors, cashflows, frequency, phases, margin_lag, thresholds, transfer_min):
    slabs, group = axes
    dates, risk, paths = factors.shape
    sets = cashflows.shape[1]
    terms = frequency.shape[0]
    half = (terms + sets) // 2
    anywhere = pl.BlockSpec(memory_space=pltpu.HBM)
    inside = pl.BlockSpec(memory_space=pltpu.VMEM)
    dma = pltpu.SemaphoreType.DMA
    return pl.pallas_call(
        functools.partial(kernel, axes),
        out_shape=(
            jax.ShapeDtypeStruct(cashflows.shape, bf16),
            jax.ShapeDtypeStruct((dates, sets), f32),
        ),
        in_specs=[inside, anywhere] + [inside] * 5,
        out_specs=(inside, inside),
        scratch_shapes=[
            pltpu.VMEM((LAG_MAX, risk, paths), bf16),
            pltpu.VMEM((dates, sets, paths), bf16),
            pltpu.VMEM((LAG_MAX + dates, terms, paths), bf16),
            pltpu.VMEM((dates, terms + sets, terms), f32),
            pltpu.VMEM((dates, half, terms), f32),
            pltpu.VMEM((dates, half, terms), f32),
            pltpu.VMEM((group, half, terms), f32),
            pltpu.VMEM((sets, terms), bf16),
            pltpu.VMEM((LAG_MAX + dates, sets, terms), bf16),
            pltpu.VMEM((dates, sets), f32),
            pltpu.VMEM((group, dates, sets), f32),
            dma((dates,)),
            dma,
            dma,
            dma((dates,)),
            dma((dates,)),
            dma((dates,)),
            dma((group,)),
            dma((2 * group,)),
            dma((LAG_MAX + dates,)),
            dma((group,)),
            dma((group,)),
        ],
        compiler_params=pltpu.CompilerParams(
            collective_id=0, has_side_effects=True, vmem_limit_bytes=48 * 1024 * 1024
        ),
    )(
        factors,
        cashflows,
        frequency.T,
        phases.reshape(1, terms),
        margin_lag.reshape(1, sets),
        thresholds.reshape(1, sets),
        transfer_min.reshape(1, sets),
    )


def solution(mesh):
    axes = (mesh.shape["date"], mesh.shape["path"])
    return jax.shard_map(
        functools.partial(local, axes),
        mesh=mesh,
        in_specs=(P("date", None, "path"), P("date", None, "path"), P(), P(), P(), P(), P()),
        out_specs=(P("date", None, "path"), P("date", None)),
        check_vma=False,
    )
```

time: 170 us -> 49.2 us (0.29); the launches traced: 168 us -> 49 us
  waiting for transfers between devices: 58.2 us -> 0 us
  matrix products: 32.3 us -> 0 us
  blocking collectives: 15.6 us -> 0 us
  between operations: 14.1 us -> 0.65 us
  Pallas kernels: 30.9 us -> 41.2 us
  other arithmetic: 8.53 us -> 0 us
  starting transfers between devices: 6.42 us -> 0 us
  local copies, waits for them, and re-layouts: 1.84 us -> 7.13 us
    psum x1 -> x0, waiting for transfers between devices: 58.2 us -> none  [local(): gram_sum, right_sum = lax.psum((gram_sum, right_sum), 'path')]
    dot_general x5 -> x0, matrix products: 32.3 us -> none  [the longest x1 11.6 us: featurize(): jnp.einsum('kr,trp->tkp', frequency, factors, preferred_element_type=jnp....]
    psum x1 -> x0, blocking collectives: 15.6 us -> none  [local(): profile = lax.psum(jnp.sum(exposure, axis=2), 'path') / paths_all]
    pallas_call x1, Pallas kernels: 30.9 us -> 41.2 us  [local(): pl.pallas_call(functools.partial(kernel, axes), out_shape=(jax.ShapeDtype...]
    reduce_sum x1 -> x0, other arithmetic: 7.92 us -> none  [local(): profile = lax.psum(jnp.sum(exposure, axis=2), 'path') / paths_all]
    unnamed x12 -> x14, local copies, waits for them, and re-layouts: 0.03 us -> 7.13 us
    ppermute x2 -> x0, starting transfers between devices: 6.39 us -> none  [shifted_2(): return lax.ppermute(value, axis, pairs)]
    slice x2 -> x0, local copies, waits for them, and re-layouts: 1.82 us -> none  [the longest x1 0.97 us: local(): prior_factors = shifted_2(factors[-LAG_MAX:], 'date', 1)]
  transfers between devices with their start and end apart: 3 -> 0, of which waited for: 1 -> 0; matrix products, arithmetic and copies ran while one was open for 18% -> 0% of each run, Pallas kernels for 18% -> 0%
where the time goes in v1:
time: 49.2 us; the launch traced here: 49 us
  Pallas kernels  41.2 us (84%)
  local copies, waits for them, and re-layouts  7.13 us (14%)
  between operations  0.65 us (1%)
    pallas_call x1, Pallas kernels, local(): pl.pallas_call(functools.partial(kernel, axes), out_shape=(jax.ShapeDtype...  41.2 us
    unnamed x14, local copies, waits for them, and re-layouts  7.13 us

profile of v1, /device:TPU:5, one launch (start us, length us, event | category | flops | bytes accessed | tf_op | source)
XLA Modules:
  0.0 49.0 jit_solution(11216932708806698069)
XLA Ops:
  0.6 0.0 copy-start
  0.6 1.2 %copy-done = bf16[8,16,4096]{2,1,0:T(8,128)(2,1)S(1)} copy-done((bf16[8,16,4096]{2,1,0:T(8,128)(2,1)S(1)}, bf16[8,16,4096]{2,1,0:T(8,128)(2,1)}, u32[]{:S(2)}) %copy-start) | copy-done | bytes 1048600
  1.9 0.0 copy-start.1
  1.9 0.7 %copy-done.1 = bf16[128,16]{0,1:T(8,128)(2,1)S(1)} copy-done((bf16[128,16]{0,1:T(8,128)(2,1)S(1)}, bf16[128,16]{0,1:T(8,128)(2,1)}, u32[]{:S(2)}) %copy-start.1) | copy-done | bytes 4120
  2.5 0.0 copy-start.2
  2.5 0.7 %copy-done.2 = f32[128]{0:T(128)S(1)} copy-done((f32[128]{0:T(128)S(1)}, f32[128]{0:T(128)}, u32[]{:S(2)}) %copy-start.2) | copy-done | bytes 536
  3.2 0.0 copy-start.3
  3.2 0.7 %copy-done.3 = s32[64]{0:T(128)S(1)} copy-done((s32[64]{0:T(128)S(1)}, s32[64]{0:T(128)}, u32[]{:S(2)}) %copy-start.3) | copy-done | bytes 280
  3.9 0.0 copy-start.4
  3.9 0.7 %copy-done.4 = s32[64]{0:T(128)S(1)} copy-done((s32[64]{0:T(128)S(1)}, s32[64]{0:T(128)}, u32[]{:S(2)}) %copy-start.4) | copy-done | bytes 280
  4.5 0.0 copy-start.5
  4.5 0.7 %copy-done.5 = s32[64]{0:T(128)S(1)} copy-done((s32[64]{0:T(128)S(1)}, s32[64]{0:T(128)}, u32[]{:S(2)}) %copy-start.5) | copy-done | bytes 280
  5.2 41.2 %shard_map.86 = (bf16[8,64,4096]{2,1,0:T(8,128)(2,1)S(1)}, f32[8,64]{1,0:T(8,128)S(1)}) custom-call(bf16[8,16,4096]{2,1,0:T(8,128)(2,1)S(1)} %copy-done, bf16[8,64,4096]{2,1,0:T(8,128)(2,1)} %cashflows.1, bf16[16,128]{1,0:T(8,128)(2,1)S(1)} %bitcast.5, f32[1,128]{1,0:T(1,128)S(1)} %bitcast.6, s32[1,64]{1,0:T(1,128)S(1)} %bitcast.7, s32[1,64]{1,0:T(1,128)S(1)} %bitcast.8, ...), custom_call_target="tpu_custom_call" | custom-call | tf_op jit(solution)/shard_map/pallas_call | solution.py:477
  46.4 2.0 %copy.11 = bf16[8,64,4096]{2,1,0:T(8,128)(2,1)} copy(bf16[8,64,4096]{2,1,0:T(8,128)(2,1)S(1)} %get-tuple-element.4) | data formatting | bytes 8388608
  48.4 0.6 %copy.12 = f32[8,64]{1,0:T(8,128)} copy(f32[8,64]{1,0:T(8,128)S(1)} %get-tuple-element.5) | data formatting | bytes 4096
Async XLA Ops:
  0.6 1.2 %copy-start = (bf16[8,16,4096]{2,1,0:T(8,128)(2,1)S(1)}, bf16[8,16,4096]{2,1,0:T(8,128)(2,1)}, u32[]{:S(2)}) copy-start(bf16[8,16,4096]{2,1,0:T(8,128)(2,1)} %factors.1) | copy-start | bytes 3145732
  1.9 0.7 %copy-start.1 = (bf16[128,16]{0,1:T(8,128)(2,1)S(1)}, bf16[128,16]{0,1:T(8,128)(2,1)}, u32[]{:S(2)}) copy-start(bf16[128,16]{0,1:T(8,128)(2,1)} %param.9) | copy-start | bytes 12292
  2.5 0.7 %copy-start.2 = (f32[128]{0:T(128)S(1)}, f32[128]{0:T(128)}, u32[]{:S(2)}) copy-start(f32[128]{0:T(128)} %param.10) | copy-start | bytes 1540
  3.2 0.7 %copy-start.3 = (s32[64]{0:T(128)S(1)}, s32[64]{0:T(128)}, u32[]{:S(2)}) copy-start(s32[64]{0:T(128)} %param.11) | copy-start | bytes 772
  3.9 0.7 %copy-start.4 = (s32[64]{0:T(128)S(1)}, s32[64]{0:T(128)}, u32[]{:S(2)}) copy-start(s32[64]{0:T(128)} %param.12) | copy-start | bytes 772
  4.5 0.7 %copy-start.5 = (s32[64]{0:T(128)S(1)}, s32[64]{0:T(128)}, u32[]{:S(2)}) copy-start(s32[64]{0:T(128)} %param.13) | copy-start | bytes 772

commit v2 on v1

--- a/solution.py
+++ b/solution.py
@@ -17,8 +17,10 @@
 root_two = 1.4142135623730951
 half_wave = (1.6817899533136271, -8.29873762982186, 6.809195244612708, -2.0985399883857303)
 newton_steps = 8
-FEATURE_WIDTH = 512
-VALUE_WIDTH = 512
+FEATURE_WIDTH = 2048
+VALUE_WIDTH = 1024
+EXPOSE_WIDTH = 512
+VMEM_LIMIT = 60751872
 
 
 def split(x, parts):
@@ -87,15 +89,21 @@
 
 def kernel(
     axes,
-    factors,
+    factors_far,
     cashflows,
+    frequency_far,
+    phases_far,
+    margin_lag_far,
+    thresholds_far,
+    transfer_min_far,
+    exposure,
+    profile,
     frequency,
     phases,
     margin_lag,
     thresholds,
     transfer_min,
-    exposure,
-    profile,
+    factors,
     state,
     flows,
     features,
@@ -107,6 +115,10 @@
     coefficients,
     profile_own,
     profile_all,
+    values,
+    totals,
+    small_sem,
+    state_sem,
     flows_sem,
     prior_send,
     prior_recv,
@@ -120,7 +132,7 @@
     profile_recv,
 ):
     slabs, group = axes
-    dates, risk, paths = factors.shape
+    dates, risk, paths = factors_far.shape
     terms = frequency.shape[1]
     sets = cashflows.shape[1]
     half = (terms + sets) // 2
@@ -166,13 +178,36 @@
             cashflows.at[date_at(step)], flows.at[step], flows_sem.at[step]
         )
 
+    def state_copy(step):
+        return pltpu.make_async_copy(
+            factors_far.at[date_at(step)], factors.at[step], state_sem.at[step]
+        )
+
+    small = [
+        pltpu.make_async_copy(source, target, small_sem.at[i])
+        for i, (source, target) in enumerate(
+            (
+                (frequency_far, frequency),
+                (phases_far, phases),
+                (margin_lag_far, margin_lag),
+                (thresholds_far, thresholds),
+                (transfer_min_far, transfer_min),
+            )
+        )
+    ]
+    for copy in small:
+        copy.start()
+
     def load(step, carry):
+        state_copy(step).start()
         flows_copy(step).start()
         return carry
 
     lax.fori_loop(0, dates, load, 0)
     lax.fori_loop(0, group, greet, 0)
 
+    for copy in small:
+        copy.wait()
     turn = split(frequency[...].astype(f32).T * inverse_turn, 3)
     phase = split(as_column(phases[...] * inverse_turn, terms), 3)
     lane = lax.broadcasted_iota(jnp.int32, (terms, risk), 1)
@@ -232,7 +267,7 @@
 
     def prior_copy(target):
         return pltpu.make_async_remote_copy(
-            src_ref=factors.at[pl.ds(dates - LAG_MAX, LAG_MAX)],
+            src_ref=factors_far.at[pl.ds(dates - LAG_MAX, LAG_MAX)],
             dst_ref=state,
             send_sem=prior_send,
             recv_sem=prior_recv,
@@ -244,7 +279,7 @@
         slot = LAG_MAX + step
         total = None
         for column in range(0, paths, FEATURE_WIDTH):
-            featurize(factors, date_at(step), slot, column)
+            featurize(factors, step, slot, column)
             columns = pl.ds(column, FEATURE_WIDTH)
             now = features[slot, :, columns]
             both = jnp.concatenate([now, flows[step, :, columns]], axis=0)
@@ -253,6 +288,7 @@
         partial_sum[step] = total
 
     def forward(step, carry):
+        state_copy(step).wait()
         flows_copy(step).wait()
         gram(step)
 
@@ -261,6 +297,10 @@
             neighbours = (slab + slabs - 1) // slabs + (2 * slabs - 2 - slab) // slabs
             pl.semaphore_wait(barrier, group - 1 + group * neighbours)
 
+            @pl.when(has_next)
+            def _():
+                prior_copy(slab + 1).start()
+
         pair_copy(step).start()
 
         @pl.when(step > 0)
@@ -270,10 +310,6 @@
         return carry
 
     lax.fori_loop(0, dates, forward, 0)
-
-    @pl.when(has_next)
-    def _():
-        prior_copy(slab + 1).start()
 
     deliver(dates - 1)
 
@@ -288,26 +324,34 @@
 
         lax.fori_loop(0, LAG_MAX, prior, 0)
 
-    @pl.when(jnp.logical_not(has_prior))
-    def _():
-        features[pl.ds(0, LAG_MAX)] = jnp.zeros((LAG_MAX,) + features.shape[1:], bf16)
-        coefficients[pl.ds(0, LAG_MAX)] = jnp.zeros((LAG_MAX, sets, terms), bf16)
-
-    def coefficients_copy(target, j, slot, sem):
+    def coefficients_copy(source, slab_index, path_index, slot, sem):
         return pltpu.make_async_remote_copy(
-            src_ref=own_coefficients,
+            src_ref=source,
             dst_ref=coefficients.at[slot],
             send_sem=coefficients_send.at[sem],
             recv_sem=coefficients_recv.at[slot],
-            device_id=device(target, j),
+            device_id=device(slab_index, path_index),
             device_id_type=MESH,
         )
 
     own = lax.div(me, spread)
     is_owner = lax.rem(me, spread) == 0
-    tell_next = jnp.logical_and(
-        jnp.logical_and(is_owner, has_next), own >= dates - LAG_MAX
-    )
+    chips = group // 2
+    chip = lax.div(me, 2)
+    relay = chips
+    onward = chips + dates
+
+    def evaluate(slot, feature_slot):
+        for column in range(0, paths, VALUE_WIDTH):
+            columns = pl.ds(column, VALUE_WIDTH)
+            value = contract(coefficients[slot], features[feature_slot, :, columns])
+            values[slot, :, columns] = value.astype(bf16)
+
+    def pass_on(source, date):
+        @pl.when(jnp.logical_and(has_next, date >= dates - LAG_MAX))
+        def _():
+            slot = date - (dates - LAG_MAX)
+            coefficients_copy(source, slab + 1, me, slot, onward + slot).start()
 
     @pl.when(is_owner)
     def _():
@@ -332,71 +376,97 @@
         own_coefficients[...] = answer
         coefficients[LAG_MAX + own] = answer
 
-        def tell(j, carry):
-            @pl.when(j != me)
+        def tell(distance, carry):
+            for there in (chip + distance, chip - distance):
+
+                @pl.when(jnp.logical_and(there >= 0, there < chips))
+                def _():
+                    coefficients_copy(
+                        own_coefficients, slab, 2 * there + side, LAG_MAX + own, there
+                    ).start()
+
+            return carry
+
+        lax.fori_loop(1, chips, tell, 0)
+        coefficients_copy(own_coefficients, slab, partner, LAG_MAX + own, chip).start()
+        pass_on(own_coefficients, own)
+        evaluate(LAG_MAX + own, LAG_MAX + step_of(own))
+
+    def visit(there, which):
+        owner = 2 * there + which
+        date = lax.div(owner, spread)
+        slot = LAG_MAX + date
+
+        @pl.when(jnp.logical_and(lax.rem(owner, spread) == 0, owner != me))
+        def _():
+            coefficients_copy(own_coefficients, slab, me, slot, 0).wait_recv()
+
+            @pl.when(jnp.logical_and(which == side, there != chip))
             def _():
-                coefficients_copy(slab, j, LAG_MAX + own, j).start()
-
-            return carry
-
-        lax.fori_loop(0, group, tell, 0)
-
-    @pl.when(tell_next)
-    def _():
-        def tell(j, carry):
-            coefficients_copy(slab + 1, j, own - (dates - LAG_MAX), group + j).start()
-            return carry
-
-        lax.fori_loop(0, group, tell, 0)
-
-    def arrived_coefficients(date, carry):
-        @pl.when(date * spread != me)
-        def _():
-            coefficients_copy(slab, me, LAG_MAX + date, 0).wait_recv()
-
-        return carry
-
-    lax.fori_loop(0, dates, arrived_coefficients, 0)
+                coefficients_copy(
+                    coefficients.at[slot], slab, partner, slot, relay + date
+                ).start()
+
+            pass_on(coefficients.at[slot], date)
+            evaluate(slot, LAG_MAX + step_of(date))
+
+    visit(chip, 1 - side)
+
+    def collect(distance, carry):
+        for there in (chip + distance, chip - distance):
+
+            @pl.when(jnp.logical_and(there >= 0, there < chips))
+            def _():
+                def both(i, carry):
+                    visit(there, lax.rem(side + i, 2))
+                    return carry
+
+                lax.fori_loop(0, 2, both, 0)
+
+        return carry
+
+    lax.fori_loop(1, chips, collect, 0)
 
     @pl.when(has_prior)
     def _():
-        for i in range(LAG_MAX):
-            coefficients_copy(slab, me, i, 0).wait_recv()
+        def prior(slot, carry):
+            coefficients_copy(own_coefficients, slab, me, slot, 0).wait_recv()
+            evaluate(slot, slot)
+            return carry
+
+        lax.fori_loop(0, LAG_MAX, prior, 0)
+
+    @pl.when(jnp.logical_not(has_prior))
+    def _():
+        values[pl.ds(0, LAG_MAX)] = jnp.zeros((LAG_MAX, sets, paths), bf16)
 
     lag = as_column(margin_lag[...].astype(f32), 128)
     offset = as_column((thresholds[...] + transfer_min[...]).astype(f32) / 100.0, 128)
-    repeat = VALUE_WIDTH // 128
+    repeat = EXPOSE_WIDTH // 128
     lag = jnp.concatenate([lag] * repeat, axis=1)
     offset = jnp.concatenate([offset] * repeat, axis=1)
-
-    def expose(block, totals):
-        columns = pl.ds(pl.multiple_of(block * VALUE_WIDTH, VALUE_WIDTH), VALUE_WIDTH)
-        earlier = []
-        new_totals = []
-        for date in range(-LAG_MAX, dates):
-            slot = LAG_MAX + date if date < 0 else LAG_MAX + step_of(date)
-            value = contract(coefficients[LAG_MAX + date], features[slot, :, columns])
-            value = value.astype(bf16)
-            if date >= 0:
-                lagged = jnp.zeros(value.shape, f32)
-                for lag_value in range(1, LAG_MAX + 1):
-                    lagged = jnp.where(
-                        lag == lag_value, earlier[-lag_value].astype(f32), lagged
-                    )
-                collateral = jnp.maximum(lagged - offset, 0.0)
-                open_value = jnp.maximum(value.astype(f32) - collateral, 0.0)
-                exposure[date, :, columns] = open_value.astype(bf16)
-                total = totals[date]
-                for i in range(repeat):
-                    total = total + open_value[:, 128 * i : 128 * (i + 1)]
-                new_totals.append(total)
-            earlier.append(value)
-        return tuple(new_totals)
-
-    blocks = paths // VALUE_WIDTH
-    totals = tuple(jnp.zeros((sets, 128), f32) for _ in range(dates))
-    totals = lax.fori_loop(0, blocks, expose, totals)
-    rows = [jnp.sum(total.T, axis=0, keepdims=True) for total in totals]
+    totals[...] = jnp.zeros(totals.shape, f32)
+
+    def expose(block, carry):
+        columns = pl.ds(pl.multiple_of(block * EXPOSE_WIDTH, EXPOSE_WIDTH), EXPOSE_WIDTH)
+        earlier = [values[slot, :, columns].astype(f32) for slot in range(LAG_MAX)]
+        for date in range(dates):
+            value = values[LAG_MAX + date, :, columns].astype(f32)
+            lagged = jnp.zeros(value.shape, f32)
+            for lag_value in range(1, LAG_MAX + 1):
+                lagged = jnp.where(lag == lag_value, earlier[-lag_value], lagged)
+            collateral = jnp.maximum(lagged - offset, 0.0)
+            open_value = jnp.maximum(value - collateral, 0.0)
+            exposure[date, :, columns] = open_value.astype(bf16)
+            total = open_value[:, :128]
+            for i in range(1, repeat):
+                total = total + open_value[:, 128 * i : 128 * (i + 1)]
+            totals[date] = totals[date] + total
+            earlier = earlier[1:] + [value]
+        return carry
+
+    lax.fori_loop(0, paths // EXPOSE_WIDTH, expose, 0)
+    rows = [jnp.sum(totals[date].T, axis=0, keepdims=True) for date in range(dates)]
     profile_own[...] = jnp.concatenate(rows, axis=0)
 
     def profile_copy(j, slot):
@@ -448,17 +518,33 @@
         def _():
             profile_copy(j, me).wait_send()
 
-            @pl.when(is_owner)
-            def _():
-                coefficients_copy(slab, me, 0, j).wait_send()
-
-        @pl.when(tell_next)
-        def _():
-            coefficients_copy(slab, me, 0, group + j).wait_send()
-
         return carry
 
     lax.fori_loop(0, group, told, 0)
+
+    @pl.when(is_owner)
+    def _():
+        def told_chip(there, carry):
+            coefficients_copy(own_coefficients, slab, me, 0, there).wait_send()
+            return carry
+
+        lax.fori_loop(0, chips, told_chip, 0)
+
+    def relayed(date, carry):
+        owner = date * spread
+
+        @pl.when(jnp.logical_and(lax.rem(owner, 2) == side, lax.div(owner, 2) != chip))
+        def _():
+            coefficients_copy(own_coefficients, slab, me, 0, relay + date).wait_send()
+
+        return carry
+
+    lax.fori_loop(0, dates, relayed, 0)
+
+    @pl.when(has_next)
+    def _():
+        for slot in range(LAG_MAX):
+            coefficients_copy(own_coefficients, slab, me, 0, onward + slot).wait_send()
 
     @pl.when(has_next)
     def _():
@@ -477,12 +563,18 @@
     return pl.pallas_call(
         functools.partial(kernel, axes),
         out_shape=(
-            jax.ShapeDtypeStruct(cashflows.shape, bf16),
+            pltpu.VMEM(cashflows.shape, bf16),
             jax.ShapeDtypeStruct((dates, sets), f32),
         ),
-        in_specs=[inside, anywhere] + [inside] * 5,
+        in_specs=[anywhere] * 7,
         out_specs=(inside, inside),
         scratch_shapes=[
+            pltpu.VMEM((risk, terms), bf16),
+            pltpu.VMEM((1, terms), f32),
+            pltpu.VMEM((1, sets), jnp.int32),
+            pltpu.VMEM((1, sets), jnp.int32),
+            pltpu.VMEM((1, sets), jnp.int32),
+            pltpu.VMEM((dates, risk, paths), bf16),
             pltpu.VMEM((LAG_MAX, risk, paths), bf16),
             pltpu.VMEM((dates, sets, paths), bf16),
             pltpu.VMEM((LAG_MAX + dates, terms, paths), bf16),
@@ -494,6 +586,10 @@
             pltpu.VMEM((LAG_MAX + dates, sets, terms), bf16),
             pltpu.VMEM((dates, sets), f32),
             pltpu.VMEM((group, dates, sets), f32),
+            pltpu.VMEM((LAG_MAX + dates, sets, paths), bf16),
+            pltpu.VMEM((dates, sets, 128), f32),
+            dma((5,)),
+            dma((dates,)),
             dma((dates,)),
             dma,
             dma,
@@ -501,13 +597,13 @@
             dma((dates,)),
             dma((dates,)),
             dma((group,)),
-            dma((2 * group,)),
+            dma((group // 2 + dates + LAG_MAX,)),
             dma((LAG_MAX + dates,)),
             dma((group,)),
             dma((group,)),
         ],
         compiler_params=pltpu.CompilerParams(
-            collective_id=0, has_side_effects=True, vmem_limit_bytes=48 * 1024 * 1024
+            collective_id=0, has_side_effects=True, vmem_limit_bytes=VMEM_LIMIT
         ),
     )(
         factors,

time: 49.2 us -> 39.2 us (0.80)
  Pallas kernels: 41.2 us -> 35.8 us
  local copies, waits for them, and re-layouts: 7.13 us -> 2.61 us
    pallas_call x1, Pallas kernels: 41.2 us -> 35.8 us  [local(): pl.pallas_call(functools.partial(kernel, axes), out_shape=(pltpu.VMEM(cas...]
    unnamed x14 -> x4, local copies, waits for them, and re-layouts: 7.13 us -> 2.61 us
where the time goes in v2:
time: 39.2 us; the launch traced here: 39.1 us
  Pallas kernels  35.8 us (91%)
  local copies, waits for them, and re-layouts  2.61 us (7%)
  between operations  0.65 us (2%)
    pallas_call x1, Pallas kernels, local(): pl.pallas_call(functools.partial(kernel, axes), out_shape=(pltpu.VMEM(cas...  35.8 us
    unnamed x4, local copies, waits for them, and re-layouts  2.61 us

profile of v2, /device:TPU:5, one launch (start us, length us, event | category | flops | bytes accessed | tf_op | source)
XLA Modules:
  0.0 39.1 jit_solution(959807687428528113)
XLA Ops:
  0.6 35.8 %shard_map.86 = (bf16[8,64,4096]{2,1,0:T(8,128)(2,1)S(1)}, f32[8,64]{1,0:T(8,128)}) custom-call(bf16[8,16,4096]{2,1,0:T(8,128)(2,1)} %factors_far.1, bf16[8,64,4096]{2,1,0:T(8,128)(2,1)} %cashflows.1, bf16[16,128]{1,0:T(8,128)(2,1)} %bitcast.5, f32[1,128]{1,0:T(1,128)} %bitcast.6, s32[1,64]{1,0:T(1,128)} %bitcast.7, s32[1,64]{1,0:T(1,128)} %bitcast.8, ...), custom_call_target="tpu_custom_call" | custom-call | tf_op jit(solution)/shard_map/pallas_call | solution.py:563
  36.4 0.0 copy-start
  36.5 2.0 %copy.11 = bf16[8,64,4096]{2,1,0:T(8,128)(2,1)} copy(bf16[8,64,4096]{2,1,0:T(8,128)(2,1)S(1)} %get-tuple-element.2) | data formatting | bytes 8388608
  38.5 0.0 copy-done
  38.5 0.6 %copy.12 = f32[8,64]{1,0:T(8,128)} copy(f32[8,64]{1,0:T(8,128)S(1)} %copy-done) | data formatting | bytes 4096
Async XLA Ops:
  36.4 2.0 %copy-start = (f32[8,64]{1,0:T(8,128)S(1)}, f32[8,64]{1,0:T(8,128)}, u32[]{:S(2)}) copy-start(f32[8,64]{1,0:T(8,128)} %get-tuple-element.7) | copy-start | bytes 6148

commit v3 on v2

--- a/solution.py
+++ b/solution.py
@@ -17,7 +17,8 @@
 root_two = 1.4142135623730951
 half_wave = (1.6817899533136271, -8.29873762982186, 6.809195244612708, -2.0985399883857303)
 newton_steps = 8
-FEATURE_WIDTH = 2048
+FEATURE_WIDTH = 512
+UNROLL = 2
 VALUE_WIDTH = 1024
 EXPOSE_WIDTH = 512
 VMEM_LIMIT = 60751872
@@ -150,11 +151,26 @@
     def device(slab_index, path_index):
         return (slab_index, path_index)
 
+    places = dates // near
+    place = first // near
+    low = 2 * place < places
+
     def date_at(step):
-        return lax.rem(first + near + step, dates)
+        turn = step // near
+        down = places - 1 - turn
+        down = jnp.where(down > place, down, down - 1)
+        up = jnp.where(turn < place, turn, turn + 1)
+        there = jnp.where(low, down, up)
+        there = jnp.where(turn == places - 1, place, there)
+        return there * near + lax.rem(step, near)
 
     def step_of(date):
-        return lax.rem(date - first - near + 2 * dates, dates)
+        there = date // near
+        down = jnp.where(there > place, places - 1 - there, places - 2 - there)
+        up = jnp.where(there < place, there, there - 1)
+        turn = jnp.where(low, down, up)
+        turn = jnp.where(there == place, places - 1, turn)
+        return turn * near + lax.rem(date, near)
 
     barrier = pltpu.get_barrier_semaphore()
 
@@ -198,12 +214,12 @@
     for copy in small:
         copy.start()
 
-    def load(step, carry):
+    def load(step):
         state_copy(step).start()
         flows_copy(step).start()
-        return carry
-
-    lax.fori_loop(0, dates, load, 0)
+
+    for step in range(min(2 * UNROLL, dates)):
+        load(step)
     lax.fori_loop(0, group, greet, 0)
 
     for copy in small:
@@ -217,17 +233,18 @@
     wave_map = jnp.concatenate([piece.astype(f32) for piece in turn] + [offset_part], axis=1)
     wave_map = wave_map.astype(bf16)
 
-    def featurize(source, date, slot, first_column):
-        columns = pl.ds(first_column, FEATURE_WIDTH)
-        now = source[date, :, columns]
+    def turns_of(source, date, first_column):
+        now = source[date, :, pl.ds(first_column, FEATURE_WIDTH)]
         stacked = jnp.concatenate([now, now, now, jnp.ones(now.shape, bf16)], axis=0)
-        turns = contract(wave_map, stacked)
+        return contract(wave_map, stacked)
+
+    def wave_of(turns):
         turns = turns - jnp.round(turns)
         square = turns * turns
         total = half_wave[-1]
         for term in half_wave[-2::-1]:
             total = total * square + term
-        features[slot, :, columns] = (total * total - root_two).astype(bf16)
+        return (total * total - root_two).astype(bf16)
 
     def pair_copy(step):
         there = pl.ds(pl.multiple_of((1 - side) * half, 8), half)
@@ -250,11 +267,18 @@
             device_id_type=MESH,
         )
 
+    def pair_sum(step):
+        here = pl.ds(pl.multiple_of(side * half, 8), half)
+        pair_copy(step).wait_recv()
+        return partial_sum[step, here] + pair_part[step]
+
     def deliver(step):
-        here = pl.ds(pl.multiple_of(side * half, 8), half)
+        pair_total[step] = pair_sum(step)
+        owner_copy(step, date_at(step) * spread, me).start()
+
+    def deliver_or_keep(step):
         owner = date_at(step) * spread
-        pair_copy(step).wait_recv()
-        total = partial_sum[step, here] + pair_part[step]
+        total = pair_sum(step)
 
         @pl.when(owner == me)
         def _():
@@ -275,43 +299,75 @@
             device_id_type=MESH,
         )
 
-    def gram(step):
-        slot = LAG_MAX + step
-        total = None
-        for column in range(0, paths, FEATURE_WIDTH):
-            featurize(factors, step, slot, column)
-            columns = pl.ds(column, FEATURE_WIDTH)
-            now = features[slot, :, columns]
-            both = jnp.concatenate([now, flows[step, :, columns]], axis=0)
-            part = contract_last(both, now)
-            total = part if total is None else total + part
-        partial_sum[step] = total
-
-    def forward(step, carry):
+    def gram(steps, done):
+        blocks = [(i, c) for i in range(len(steps)) for c in range(0, paths, FEATURE_WIDTH)]
+        sums = [None] * len(steps)
+
+        def accumulate(block, now):
+            i, column = block
+            flow = flows[steps[i], :, pl.ds(column, FEATURE_WIDTH)]
+            part = contract_last(jnp.concatenate([now, flow], axis=0), now)
+            sums[i] = part if sums[i] is None else sums[i] + part
+            if column + FEATURE_WIDTH == paths:
+                partial_sum[steps[i]] = sums[i]
+                done(i)
+
+        turns = turns_of(factors, steps[0], 0)
+        before = None
+        for n, (i, column) in enumerate(blocks):
+            following = None
+            if n + 1 < len(blocks):
+                following = turns_of(factors, steps[blocks[n + 1][0]], blocks[n + 1][1])
+            if before is not None:
+                accumulate(blocks[n - 1], before)
+            before = wave_of(turns)
+            features[LAG_MAX + steps[i], :, pl.ds(column, FEATURE_WIDTH)] = before
+            turns = following
+        accumulate(blocks[-1], before)
+
+    def ready(step):
         state_copy(step).wait()
         flows_copy(step).wait()
-        gram(step)
-
-        @pl.when(step == 0)
-        def _():
-            neighbours = (slab + slabs - 1) // slabs + (2 * slabs - 2 - slab) // slabs
-            pl.semaphore_wait(barrier, group - 1 + group * neighbours)
-
-            @pl.when(has_next)
-            def _():
-                prior_copy(slab + 1).start()
-
-        pair_copy(step).start()
-
-        @pl.when(step > 0)
-        def _():
-            deliver(step - 1)
-
-        return carry
-
-    lax.fori_loop(0, dates, forward, 0)
-
-    deliver(dates - 1)
+
+    def greeted():
+        neighbours = (slab + slabs - 1) // slabs + (2 * slabs - 2 - slab) // slabs
+        pl.semaphore_wait(barrier, group - 1 + group * neighbours)
+        pair_copy(0).start()
+
+        @pl.when(has_next)
+        def _():
+            prior_copy(slab + 1).start()
+
+    ready(0)
+    gram([0], lambda i: greeted())
+    for step in range(1, UNROLL):
+        ready(step)
+        gram([step], lambda i: pair_copy(step).start())
+
+    def forward(turn, carry):
+        steps = [UNROLL * turn + i for i in range(UNROLL)]
+
+        @pl.when(turn < dates // UNROLL - 1)
+        def _():
+            for step in steps:
+                load(step + UNROLL)
+
+        for step in steps:
+            ready(step)
+        deliver(steps[0] - UNROLL)
+
+        def done(i):
+            pair_copy(steps[i]).start()
+            if i + 1 < UNROLL:
+                deliver(steps[i + 1] - UNROLL)
+
+        gram(steps, done)
+        return carry
+
+    lax.fori_loop(1, dates // UNROLL, forward, 0)
+
+    for step in range(dates - UNROLL, dates):
+        deliver_or_keep(step)
 
     @pl.when(has_prior)
     def _():
@@ -319,7 +375,8 @@
 
         def prior(slot, carry):
             for column in range(0, paths, FEATURE_WIDTH):
-                featurize(state, slot, slot, column)
+                waves = wave_of(turns_of(state, slot, column))
+                features[slot, :, pl.ds(column, FEATURE_WIDTH)] = waves
             return carry
 
         lax.fori_loop(0, LAG_MAX, prior, 0)
@@ -412,20 +469,52 @@
 
     visit(chip, 1 - side)
 
-    def collect(distance, carry):
+    def collect(turn, carry):
+        distance = 1 + lax.rem(turn, chips - 1)
+        which = lax.rem(side + turn // (chips - 1), 2)
+
         for there in (chip + distance, chip - distance):
 
             @pl.when(jnp.logical_and(there >= 0, there < chips))
             def _():
-                def both(i, carry):
-                    visit(there, lax.rem(side + i, 2))
-                    return carry
-
-                lax.fori_loop(0, 2, both, 0)
-
-        return carry
-
-    lax.fori_loop(1, chips, collect, 0)
+                visit(there, which)
+
+        return carry
+
+    lax.fori_loop(0, 2 * (chips - 1), collect, 0)
+
+    lag = as_column(margin_lag[...].astype(f32), 128)
+    offset = as_column((thresholds[...] + transfer_min[...]).astype(f32) / 100.0, 128)
+    repeat = EXPOSE_WIDTH // 128
+    lag = jnp.concatenate([lag] * repeat, axis=1)
+    offset = jnp.concatenate([offset] * repeat, axis=1)
+    totals[...] = jnp.zeros(totals.shape, f32)
+
+    def expose(first_date, end_date):
+        def body(block, carry):
+            start = pl.multiple_of(block * EXPOSE_WIDTH, EXPOSE_WIDTH)
+            columns = pl.ds(start, EXPOSE_WIDTH)
+            earlier = [
+                values[first_date + slot, :, columns].astype(f32) for slot in range(LAG_MAX)
+            ]
+            for date in range(first_date, end_date):
+                value = values[LAG_MAX + date, :, columns].astype(f32)
+                lagged = jnp.zeros(value.shape, f32)
+                for lag_value in range(1, LAG_MAX + 1):
+                    lagged = jnp.where(lag == lag_value, earlier[-lag_value], lagged)
+                collateral = jnp.maximum(lagged - offset, 0.0)
+                open_value = jnp.maximum(value - collateral, 0.0)
+                exposure[date, :, columns] = open_value.astype(bf16)
+                total = open_value[:, :128]
+                for i in range(1, repeat):
+                    total = total + open_value[:, 128 * i : 128 * (i + 1)]
+                totals[date] = totals[date] + total
+                earlier = earlier[1:] + [value]
+            return carry
+
+        lax.fori_loop(0, paths // EXPOSE_WIDTH, body, 0)
+
+    expose(LAG_MAX, dates)
 
     @pl.when(has_prior)
     def _():
@@ -440,32 +529,7 @@
     def _():
         values[pl.ds(0, LAG_MAX)] = jnp.zeros((LAG_MAX, sets, paths), bf16)
 
-    lag = as_column(margin_lag[...].astype(f32), 128)
-    offset = as_column((thresholds[...] + transfer_min[...]).astype(f32) / 100.0, 128)
-    repeat = EXPOSE_WIDTH // 128
-    lag = jnp.concatenate([lag] * repeat, axis=1)
-    offset = jnp.concatenate([offset] * repeat, axis=1)
-    totals[...] = jnp.zeros(totals.shape, f32)
-
-    def expose(block, carry):
-        columns = pl.ds(pl.multiple_of(block * EXPOSE_WIDTH, EXPOSE_WIDTH), EXPOSE_WIDTH)
-        earlier = [values[slot, :, columns].astype(f32) for slot in range(LAG_MAX)]
-        for date in range(dates):
-            value = values[LAG_MAX + date, :, columns].astype(f32)
-            lagged = jnp.zeros(value.shape, f32)
-            for lag_value in range(1, LAG_MAX + 1):
-                lagged = jnp.where(lag == lag_value, earlier[-lag_value], lagged)
-            collateral = jnp.maximum(lagged - offset, 0.0)
-            open_value = jnp.maximum(value - collateral, 0.0)
-            exposure[date, :, columns] = open_value.astype(bf16)
-            total = open_value[:, :128]
-            for i in range(1, repeat):
-                total = total + open_value[:, 128 * i : 128 * (i + 1)]
-            totals[date] = totals[date] + total
-            earlier = earlier[1:] + [value]
-        return carry
-
-    lax.fori_loop(0, paths // EXPOSE_WIDTH, expose, 0)
+    expose(0, LAG_MAX)
     rows = [jnp.sum(totals[date].T, axis=0, keepdims=True) for date in range(dates)]
     profile_own[...] = jnp.concatenate(rows, axis=0)
 

time: 39.2 us -> 36.3 us (0.926)
  Pallas kernels: 35.8 us -> 32.9 us
    pallas_call x1, Pallas kernels: 35.8 us -> 32.9 us  [local(): pl.pallas_call(functools.partial(kernel, axes), out_shape=(pltpu.VMEM(cas...]
where the time goes in v3:
time: 36.3 us; the launch traced here: 36.2 us
  Pallas kernels  32.9 us (91%)
  local copies, waits for them, and re-layouts  2.61 us (7%)
  between operations  0.65 us (2%)
    pallas_call x1, Pallas kernels, local(): pl.pallas_call(functools.partial(kernel, axes), out_shape=(pltpu.VMEM(cas...  32.9 us
    unnamed x4, local copies, waits for them, and re-layouts  2.61 us

profile of v3, /device:TPU:5, one launch (start us, length us, event | category | flops | bytes accessed | tf_op | source)
XLA Modules:
  0.0 36.2 jit_solution(11213090795915018546)
XLA Ops:
  0.6 32.9 %shard_map.86 = (bf16[8,64,4096]{2,1,0:T(8,128)(2,1)S(1)}, f32[8,64]{1,0:T(8,128)}) custom-call(bf16[8,16,4096]{2,1,0:T(8,128)(2,1)} %factors_far.1, bf16[8,64,4096]{2,1,0:T(8,128)(2,1)} %cashflows.1, bf16[16,128]{1,0:T(8,128)(2,1)} %bitcast.5, f32[1,128]{1,0:T(1,128)} %bitcast.6, s32[1,64]{1,0:T(1,128)} %bitcast.7, s32[1,64]{1,0:T(1,128)} %bitcast.8, ...), custom_call_target="tpu_custom_call" | custom-call | tf_op jit(solution)/shard_map/pallas_call | solution.py:627
  33.5 0.0 copy-start
  33.5 2.0 %copy.11 = bf16[8,64,4096]{2,1,0:T(8,128)(2,1)} copy(bf16[8,64,4096]{2,1,0:T(8,128)(2,1)S(1)} %get-tuple-element.2) | data formatting | bytes 8388608
  35.6 0.0 copy-done
  35.6 0.6 %copy.12 = f32[8,64]{1,0:T(8,128)} copy(f32[8,64]{1,0:T(8,128)S(1)} %copy-done) | data formatting | bytes 4096
Async XLA Ops:
  33.5 2.0 %copy-start = (f32[8,64]{1,0:T(8,128)S(1)}, f32[8,64]{1,0:T(8,128)}, u32[]{:S(2)}) copy-start(f32[8,64]{1,0:T(8,128)} %get-tuple-element.7) | copy-start | bytes 6148

commit v4 on v3

--- a/solution.py
+++ b/solution.py
@@ -118,6 +118,8 @@
     profile_all,
     values,
     totals,
+    lag_column,
+    offset_column,
     small_sem,
     state_sem,
     flows_sem,
@@ -369,17 +371,24 @@
     for step in range(dates - UNROLL, dates):
         deliver_or_keep(step)
 
-    @pl.when(has_prior)
-    def _():
-        prior_copy(slab).wait_recv()
-
-        def prior(slot, carry):
+    lag_column[...] = as_column(margin_lag[...].astype(f32), 128)
+    offset_column[...] = as_column(
+        (thresholds[...] + transfer_min[...]).astype(f32) / 100.0, 128
+    )
+    totals[...] = jnp.zeros(totals.shape, f32)
+
+    def prior_features(slot):
+        @pl.when(has_prior)
+        def _():
+            if slot == 0:
+                prior_copy(slab).wait_recv()
+            turns = turns_of(state, slot, 0)
             for column in range(0, paths, FEATURE_WIDTH):
-                waves = wave_of(turns_of(state, slot, column))
-                features[slot, :, pl.ds(column, FEATURE_WIDTH)] = waves
-            return carry
-
-        lax.fori_loop(0, LAG_MAX, prior, 0)
+                following = None
+                if column + FEATURE_WIDTH < paths:
+                    following = turns_of(state, slot, column + FEATURE_WIDTH)
+                features[slot, :, pl.ds(column, FEATURE_WIDTH)] = wave_of(turns)
+                turns = following
 
     def coefficients_copy(source, slab_index, path_index, slot, sem):
         return pltpu.make_async_remote_copy(
@@ -433,7 +442,8 @@
         own_coefficients[...] = answer
         coefficients[LAG_MAX + own] = answer
 
-        def tell(distance, carry):
+        def tell(turn, carry):
+            distance = chips - turn
             for there in (chip + distance, chip - distance):
 
                 @pl.when(jnp.logical_and(there >= 0, there < chips))
@@ -467,7 +477,10 @@
             pass_on(coefficients.at[slot], date)
             evaluate(slot, LAG_MAX + step_of(date))
 
+    prior_features(0)
     visit(chip, 1 - side)
+    for slot in range(1, LAG_MAX):
+        prior_features(slot)
 
     def collect(turn, carry):
         distance = 1 + lax.rem(turn, chips - 1)
@@ -483,14 +496,12 @@
 
     lax.fori_loop(0, 2 * (chips - 1), collect, 0)
 
-    lag = as_column(margin_lag[...].astype(f32), 128)
-    offset = as_column((thresholds[...] + transfer_min[...]).astype(f32) / 100.0, 128)
     repeat = EXPOSE_WIDTH // 128
-    lag = jnp.concatenate([lag] * repeat, axis=1)
-    offset = jnp.concatenate([offset] * repeat, axis=1)
-    totals[...] = jnp.zeros(totals.shape, f32)
 
     def expose(first_date, end_date):
+        lag = jnp.concatenate([lag_column[...]] * repeat, axis=1)
+        offset = jnp.concatenate([offset_column[...]] * repeat, axis=1)
+
         def body(block, carry):
             start = pl.multiple_of(block * EXPOSE_WIDTH, EXPOSE_WIDTH)
             columns = pl.ds(start, EXPOSE_WIDTH)
@@ -652,6 +663,8 @@
             pltpu.VMEM((group, dates, sets), f32),
             pltpu.VMEM((LAG_MAX + dates, sets, paths), bf16),
             pltpu.VMEM((dates, sets, 128), f32),
+            pltpu.VMEM((sets, 128), f32),
+            pltpu.VMEM((sets, 128), f32),
             dma((5,)),
             dma((dates,)),
             dma((dates,)),

time: 36.3 us -> 35.7 us (0.983)
  the two profiles are of different devices: /device:TPU:5 before, /device:TPU:0 now
where the time goes in v4:
time: 35.7 us; the launch traced here: 35.5 us
  Pallas kernels  32.3 us (90%)
  local copies, waits for them, and re-layouts  2.61 us (7%)
  between operations  0.65 us (2%)
    pallas_call x1, Pallas kernels, local(): pl.pallas_call(functools.partial(kernel, axes), out_shape=(pltpu.VMEM(cas...  32.3 us
    unnamed x4, local copies, waits for them, and re-layouts  2.61 us

profile of v4, /device:TPU:0, one launch (start us, length us, event | category | flops | bytes accessed | tf_op | source)
XLA Modules:
  0.0 35.5 jit_solution(10154472793930088624)
XLA Ops:
  0.6 32.3 %shard_map.86 = (bf16[8,64,4096]{2,1,0:T(8,128)(2,1)S(1)}, f32[8,64]{1,0:T(8,128)}) custom-call(bf16[8,16,4096]{2,1,0:T(8,128)(2,1)} %factors_far.1, bf16[8,64,4096]{2,1,0:T(8,128)(2,1)} %cashflows.1, bf16[16,128]{1,0:T(8,128)(2,1)} %bitcast.5, f32[1,128]{1,0:T(1,128)} %bitcast.6, s32[1,64]{1,0:T(1,128)} %bitcast.7, s32[1,64]{1,0:T(1,128)} %bitcast.8, ...), custom_call_target="tpu_custom_call" | custom-call | tf_op jit(solution)/shard_map/pallas_call | solution.py:638
  32.9 0.0 copy-start
  32.9 2.0 %copy.11 = bf16[8,64,4096]{2,1,0:T(8,128)(2,1)} copy(bf16[8,64,4096]{2,1,0:T(8,128)(2,1)S(1)} %get-tuple-element.2) | data formatting | bytes 8388608
  34.9 0.0 copy-done
  35.0 0.6 %copy.12 = f32[8,64]{1,0:T(8,128)} copy(f32[8,64]{1,0:T(8,128)S(1)} %copy-done) | data formatting | bytes 4096
Async XLA Ops:
  32.9 2.0 %copy-start = (f32[8,64]{1,0:T(8,128)S(1)}, f32[8,64]{1,0:T(8,128)}, u32[]{:S(2)}) copy-start(f32[8,64]{1,0:T(8,128)} %get-tuple-element.7) | copy-start | bytes 6148
